TPU v7x, 128 devices: a whole 4x4x4 slice. The times are simulated.
128 devices in a mesh: freq: 4 (over y), pts: 32 (over z, x, core).
Axes of the slice: x: 4, y: 4, z: 4, core: 2. Of those that a mesh axis runs over, the one named last changes fastest.
Arguments:
- data: float32 [2, 32, 64, 3, 32768], P(None, 'freq', None, None, 'pts'), may hold values from -180 to 180
- quad_weight: float32 [32768], P('pts'), may hold values from 0.2 to 5
- basis: float32 [2, 32, 64, 8], P(None, 'freq'), may hold values from -6 to 6
Outputs:
- basis_out: float32 [2, 32, 64, 8], P(None, 'freq')
- spectrum: float32 [32, 8], P('freq')
- modes: float32 [2, 32, 8, 3, 32768], P(None, 'freq', None, None, 'pts')
All inputs are finite; a program needn't handle non-finite values.
Results may differ from a plain program's by a relative error of at most 0.0001.
Values sent between devices are 32-bit elements; how exact they have to be, the bound alone decides.
A program may use at most 128 MiB of HBM per device.

v0:
```python
import functools
import jax
import jax.numpy as jnp
from jax import lax
from jax.experimental import pallas as pl
from jax.experimental.pallas import tpu as pltpu
from jax.sharding import PartitionSpec as P

ITERS = 4
AHEAD = 3
F32 = jnp.float32
BF16 = jnp.bfloat16
MESH = pl.DeviceIdType.MESH


def split3(value):
    first = value.astype(BF16).astype(F32)
    rest = value - first
    second = rest.astype(BF16).astype(F32)
    return first, second, rest - second


def iota(shape, dim):
    return lax.broadcasted_iota(jnp.int32, shape, dim)


def kernel(
    data, weight, basis, basis_out, spec_out, modes_out,
    xbuf, ybuf, pbuf, rbuf, zbuf, tbuf, vbuf, abuf, rmat, obuf,
    load_sem, out_sem, ps_sem, pr_sem, zs_sem, zr_sem, ts_sem, tr_sem, vs_sem, vr_sem, as_sem, ar_sem,
):
    me = lax.axis_index("pts")
    line = lax.axis_index("freq")
    z = me // 8
    q = me % 8
    x = q // 2
    core = q % 2
    sign = 1 - 2 * ((3 - x) // 3)
    near = [(2, 0), (2, 1), (sign, 0), (sign, 1), (-sign, 0), (-sign, 1), (0, 1), (0, 0)]
    freq = [((x + dx + 4) % 4) * 2 + (core + dc) % 2 for dx, dc in near]
    rows = [z * 8 + f for f in freq]
    cols = [((z + d) % 4) * 8 + q for d in (2, 1, 3)]
    lines = [(line + d) % 4 for d in (2, 1, 3)]

    def load(s, part):
        return pltpu.make_async_copy(data.at[part, freq[s]], xbuf.at[s, part], load_sem.at[s, part])

    for s in range(AHEAD):
        load(s, 0).start()
        load(s, 1).start()

    barrier = pltpu.get_barrier_semaphore()
    for peer in rows[:7] + cols:
        pl.semaphore_signal(barrier, inc=1, device_id={"pts": peer}, device_id_type=MESH)
    for peer in lines:
        pl.semaphore_signal(barrier, inc=1, device_id={"freq": peer}, device_id_type=MESH)

    w = weight[...]
    root = jnp.sqrt(w)
    low = iota((1, 128), 1) < 64
    half = jnp.where(low, 1.0, -1.0).astype(F32)

    def product(s):
        load(s, 0).wait()
        load(s, 1).wait()
        if s + AHEAD < 8:
            load(s + AHEAD, 0).start()
            load(s + AHEAD, 1).start()
        for c in range(3):
            span = pl.ds(c * 1024, 1024)
            for part in range(2):
                y = xbuf[s, part, c] * root
                hi = y.astype(BF16)
                lo = (y - hi.astype(F32)).astype(BF16)
                ybuf[s, pl.ds(part * 64, 64), span] = hi
                ybuf[s, pl.ds(128 + part * 64, 64), span] = lo
        total = None
        for k in range(2):
            both = ybuf[s, :, pl.ds(k * 1536, 1536)]
            m = lax.dot_general(both, both, (((1,), (1,)), ((), ())), preferred_element_type=F32)
            total = m if total is None else total + m
        return (total[:128, :128] + total[128:, 128:]) + (total[:128, 128:] + total[128:, :128])

    def packed(m):
        top, bottom = m[:64], m[64:]
        straight = top + half * pltpu.roll(bottom, 64, 1)
        swapped = pltpu.roll(top, 64, 1) - half * bottom
        row = iota((64, 128), 0)
        col = iota((64, 128), 1) % 64
        upper = jnp.where(low == (col >= row), straight, swapped)
        return jnp.where(low, upper[:32], upper[32:])

    def send_product(s):
        return pltpu.make_async_remote_copy(
            src_ref=pbuf.at[s], dst_ref=rbuf.at[q], send_sem=ps_sem.at[s], recv_sem=pr_sem.at[q],
            device_id={"pts": rows[s]}, device_id_type=MESH)

    def take_product(s):
        return pltpu.make_async_remote_copy(
            src_ref=pbuf.at[s], dst_ref=rbuf.at[freq[s]], send_sem=ps_sem.at[s], recv_sem=pr_sem.at[freq[s]],
            device_id={"pts": rows[s]}, device_id_type=MESH)

    before = None
    for s in range(8):
        now = product(s)
        if s == 1:
            pl.semaphore_wait(barrier, 13)
        if s:
            pbuf[s - 1] = packed(before)
            send_product(s - 1).start()
        before = now
    total = packed(before)
    for s in range(7):
        take_product(s).wait_recv()
        total = total + rbuf[freq[s]]
    zbuf[z] = total

    def send_sum(i):
        return pltpu.make_async_remote_copy(
            src_ref=zbuf.at[z], dst_ref=zbuf.at[z], send_sem=zs_sem.at[i], recv_sem=zr_sem.at[z],
            device_id={"pts": cols[i]}, device_id_type=MESH)

    def take_sum(i):
        other = cols[i] // 8
        return pltpu.make_async_remote_copy(
            src_ref=zbuf.at[z], dst_ref=zbuf.at[other], send_sem=zs_sem.at[i], recv_sem=zr_sem.at[other],
            device_id={"pts": cols[i]}, device_id_type=MESH)

    for i in range(3):
        send_sum(i).start()
    for i in (1, 2, 0):
        take_sum(i).wait_recv()
    gram = ((zbuf[0] + zbuf[1]) + (zbuf[2] + zbuf[3])) * (1.0 / 98304.0)

    turned = pltpu.roll(gram, 64, 1)
    upper = jnp.concatenate([jnp.where(low, gram, turned), jnp.where(low, turned, gram)], axis=0)
    flipped = jnp.concatenate([upper, upper], axis=0).T[:64]
    row = iota((64, 128), 0)
    col = iota((64, 128), 1) % 64
    real = jnp.where(col >= row, upper, flipped)
    imag = jnp.where(col < row, upper, jnp.where(col > row, -flipped, 0.0))
    full = jnp.concatenate([jnp.where(low, real, -imag), jnp.where(low, imag, real)], axis=0)
    r0, r1, r2 = split3(full)
    rmat[pl.ds(0, 128), pl.ds(0, 128)] = r0.astype(BF16)
    rmat[pl.ds(128, 128), pl.ds(0, 128)] = r1.astype(BF16)
    rmat[pl.ds(0, 128), pl.ds(128, 128)] = r2.astype(BF16)
    rmat[pl.ds(128, 128), pl.ds(128, 128)] = jnp.zeros((128, 128), BF16)

    diag = jnp.where((col == row) & low, upper, 0.0)
    trace = jnp.sum(jnp.sum(diag, axis=1, keepdims=True), axis=0, keepdims=True)
    tbuf[line] = jnp.broadcast_to(trace, (8, 128))

    def send_trace(i):
        return pltpu.make_async_remote_copy(
            src_ref=tbuf.at[line], dst_ref=tbuf.at[line], send_sem=ts_sem.at[i], recv_sem=tr_sem.at[line],
            device_id={"freq": lines[i]}, device_id_type=MESH)

    def take_trace(i):
        return pltpu.make_async_remote_copy(
            src_ref=tbuf.at[line], dst_ref=tbuf.at[lines[i]], send_sem=ts_sem.at[i], recv_sem=tr_sem.at[lines[i]],
            device_id={"freq": lines[i]}, device_id_type=MESH)

    for i in range(3):
        send_trace(i).start()

    def applied(vectors):
        pieces = []
        for v in vectors:
            pieces.extend(split3(v))
        while len(pieces) % 2:
            pieces.append(jnp.zeros((8, 128), F32))
        left = jnp.concatenate(pieces, axis=0).astype(BF16)
        out = jnp.dot(jnp.concatenate([left, left], axis=1), rmat[...], preferred_element_type=F32)
        results = []
        for i in range(len(vectors)):
            parts = [out[24 * i + 8 * k : 24 * i + 8 * k + 8] for k in range(3)]
            small = (parts[2][:, :128] + parts[0][:, 128:]) + (parts[1][:, 128:] + parts[2][:, 128:])
            results.append(parts[0][:, :128] + (parts[1][:, :128] + small))
        return results

    rank = iota((8, 128), 0)
    v = jnp.concatenate([basis[0, q], basis[1, q]], axis=1)
    iv = pltpu.roll(v, 64, 1) * -half
    for step in range(ITERS):
        zv, wv = applied([v, iv])
        scale = jnp.zeros((8, 128), F32)
        for j in range(8):
            zj = jnp.broadcast_to(zv[j : j + 1], (8, 128))
            wj = jnp.broadcast_to(wv[j : j + 1], (8, 128))
            dot_real = jnp.broadcast_to(jnp.sum(zj * zv, axis=1, keepdims=True), (8, 128))
            norm = jnp.broadcast_to(dot_real[j : j + 1], (8, 128))
            factor = lax.rsqrt(norm * (1.0 / 64) + 1e-06)
            scale = jnp.where(rank == j, factor, scale)
            if j < 7:
                dot_imag = jnp.broadcast_to(jnp.sum(wj * zv, axis=1, keepdims=True), (8, 128))
                inverse = jnp.where(rank > j, factor * factor * (1.0 / 64), 0.0)
                coef_real = dot_real * inverse
                coef_imag = dot_imag * inverse
                zv, wv = (
                    zv - (coef_real * zj + coef_imag * wj),
                    wv - (coef_real * wj - coef_imag * zj),
                )
        v = zv * scale
        iv = wv * scale
    vbuf[q] = v

    def send_basis(s):
        return pltpu.make_async_remote_copy(
            src_ref=vbuf.at[q], dst_ref=vbuf.at[q], send_sem=vs_sem.at[s], recv_sem=vr_sem.at[q],
            device_id={"pts": rows[s]}, device_id_type=MESH)

    def take_basis(s):
        return pltpu.make_async_remote_copy(
            src_ref=vbuf.at[q], dst_ref=vbuf.at[freq[s]], send_sem=vs_sem.at[s], recv_sem=vr_sem.at[freq[s]],
            device_id={"pts": rows[s]}, device_id_type=MESH)

    for s in range(7):
        send_basis(s).start()

    def send_aux(s):
        return pltpu.make_async_remote_copy(
            src_ref=abuf.at[q], dst_ref=abuf.at[q], send_sem=as_sem.at[s], recv_sem=ar_sem.at[q],
            device_id={"pts": rows[s]}, device_id_type=MESH)

    def take_aux(s):
        return pltpu.make_async_remote_copy(
            src_ref=abuf.at[q], dst_ref=abuf.at[freq[s]], send_sem=as_sem.at[s], recv_sem=ar_sem.at[freq[s]],
            device_id={"pts": rows[s]}, device_id_type=MESH)

    (zv,) = applied([v])
    rayleigh = jnp.sum(v * zv, axis=1, keepdims=True) * (1.0 / 64)
    spread = jnp.sum(jnp.where(rank == iota((8, 128), 1), rayleigh, 0.0), axis=0, keepdims=True)
    for i in (1, 2, 0):
        take_trace(i).wait_recv()
    group = (tbuf[0] + tbuf[1]) + (tbuf[2] + tbuf[3])
    abuf[q] = jnp.where(rank == 0, spread, group)
    for s in range(7):
        send_aux(s).start()

    undo = lax.rsqrt(w) * (1.0 / 64)

    def store(s, part):
        return pltpu.make_async_copy(obuf.at[s, part], modes_out.at[part, freq[s]], out_sem.at[s, part])

    for s in reversed(range(8)):
        if s < 7:
            take_basis(s).wait_recv()
        vec = vbuf[freq[s]]
        other = pltpu.roll(vec, 64, 1)
        basis_out[0, freq[s]] = vec[:, :64]
        basis_out[1, freq[s]] = other[:, :64]
        left = jnp.concatenate([vec * half, other], axis=0)
        left_hi = left.astype(BF16)
        left_lo = (left - left_hi.astype(F32)).astype(BF16)
        left = jnp.concatenate([left_hi, left_lo], axis=0)
        left = jnp.concatenate([left, left], axis=1)
        for c in range(3):
            out = jnp.dot(left, ybuf[s, :, pl.ds(c * 1024, 1024)], preferred_element_type=F32)
            out = (out[:16] + out[16:]) * undo
            obuf[s, 0, c] = out[:8]
            obuf[s, 1, c] = out[8:]
        store(s, 0).start()
        store(s, 1).start()

    for s in range(7):
        take_aux(s).wait_recv()
    total = jnp.zeros((1, 128), F32)
    for f in range(8):
        total = total + abuf[f, 1:2]
    for f in range(8):
        spec_out[pl.ds(f, 1), :] = (abuf[f, 0:1] * 2048.0 / total)[:, :8]

    for s in range(7):
        send_product(s).wait_send()
        send_basis(s).wait_send()
        send_aux(s).wait_send()
    for i in range(3):
        send_sum(i).wait_send()
        send_trace(i).wait_send()
    for s in range(8):
        store(s, 0).wait()
        store(s, 1).wait()


def per_device(data, quad_weight, basis):
    data = jnp.transpose(data, (0, 1, 3, 2, 4))
    basis = jnp.transpose(basis, (0, 1, 3, 2))
    vmem = pl.BlockSpec(memory_space=pltpu.VMEM)
    hbm = pl.BlockSpec(memory_space=pl.ANY)
    dma = pltpu.SemaphoreType.DMA
    basis_out, spectrum, modes = pl.pallas_call(
        kernel,
        out_shape=(
            jax.ShapeDtypeStruct((2, 8, 8, 64), F32),
            jax.ShapeDtypeStruct((8, 8), F32),
            jax.ShapeDtypeStruct((2, 8, 3, 8, 1024), F32),
        ),
        in_specs=[hbm, vmem, vmem],
        out_specs=(vmem, vmem, hbm),
        scratch_shapes=[
            pltpu.VMEM((8, 2, 3, 64, 1024), F32),
            pltpu.VMEM((8, 256, 3072), BF16),
            pltpu.VMEM((7, 32, 128), F32),
            pltpu.VMEM((8, 32, 128), F32),
            pltpu.VMEM((4, 32, 128), F32),
            pltpu.VMEM((4, 8, 128), F32),
            pltpu.VMEM((8, 8, 128), F32),
            pltpu.VMEM((8, 8, 128), F32),
            pltpu.VMEM((256, 256), BF16),
            pltpu.VMEM((8, 2, 3, 8, 1024), F32),
            dma((8, 2)), dma((8, 2)), dma((7,)), dma((8,)), dma((3,)), dma((4,)),
            dma((3,)), dma((4,)), dma((7,)), dma((8,)), dma((7,)), dma((8,)),
        ],
        compiler_params=pltpu.CompilerParams(
            collective_id=0, has_side_effects=True, vmem_limit_bytes=48 * 1024 * 1024
        ),
        name="spod",
    )(data, quad_weight.reshape(1, -1), basis)
    return (
        jnp.transpose(basis_out, (0, 1, 3, 2)),
        spectrum,
        jnp.transpose(modes, (0, 1, 3, 2, 4)),
    )


def solution(mesh):
    in_specs = (P(None, "freq", None, None, "pts"), P("pts"), P(None, "freq", None, None))
    out_specs = (P(None, "freq", None, None), P("freq", None), P(None, "freq", None, None, "pts"))
    return jax.shard_map(
        per_device, mesh=mesh, in_specs=in_specs, out_specs=out_specs, check_vma=False
    )
```

profile of v0, /device:TPU:1, one launch (start us, length us, event | category | flops | bytes accessed | tf_op | source)
XLA Modules:
  0.0 34.2 jit_solution(15019630891657794415)
XLA Ops:
  0.6 0.0 copy-start
  0.6 0.8 %copy-done = f32[2,8,64,8]{2,3,1,0:T(8,128)S(1)} copy-done((f32[2,8,64,8]{2,3,1,0:T(8,128)S(1)}, f32[2,8,64,8]{2,3,1,0:T(8,128)}, u32[]{:S(2)}) %copy-start) | copy-done | bytes 32792
  1.5 0.0 copy-start.1
  1.5 0.7 %copy-done.1 = f32[1024]{0:T(1024)S(1)} copy-done((f32[1024]{0:T(1024)S(1)}, f32[1024]{0:T(1024)}, u32[]{:S(2)}) %copy-start.1) | copy-done | bytes 4120
  2.2 29.7 %spod.1 = (f32[2,8,8,64]{3,2,1,0:T(8,128)S(1)}, f32[8,8]{1,0:T(8,128)S(1)}, f32[2,8,3,8,1024]{4,3,2,1,0:T(8,128)S(1)}) custom-call(f32[2,8,3,64,1024]{4,3,2,1,0:T(8,128)} %bitcast.9, f32[1,1024]{1,0:T(1,128)S(1)} %bitcast.8, f32[2,8,8,64]{3,2,1,0:T(8,128)S(1)} %bitcast.6), custom_call_target="tpu_custom_call" | custom-call | tf_op jit(solution)/shard_map/spod/pallas_call | solution.py:291
  31.9 0.6 %copy.9 = f32[2,8,64,8]{2,3,1,0:T(8,128)} copy(f32[2,8,64,8]{2,3,1,0:T(8,128)S(1)} %bitcast.7) | data formatting | bytes 65536
  32.5 0.6 %copy.10 = f32[8,8]{1,0:T(8,128)} copy(f32[8,8]{1,0:T(8,128)S(1)} %get-tuple-element.13) | data formatting | bytes 512
  33.1 1.1 %copy.11 = f32[2,8,8,3,1024]{4,2,3,1,0:T(8,128)} copy(f32[2,8,8,3,1024]{4,2,3,1,0:T(8,128)S(1)} %bitcast.5) | data formatting | bytes 3145728
Async XLA Ops:
  0.6 0.8 %copy-start = (f32[2,8,64,8]{2,3,1,0:T(8,128)S(1)}, f32[2,8,64,8]{2,3,1,0:T(8,128)}, u32[]{:S(2)}) copy-start(f32[2,8,64,8]{2,3,1,0:T(8,128)} %param.5) | copy-start | bytes 98308
  1.5 0.7 %copy-start.1 = (f32[1024]{0:T(1024)S(1)}, f32[1024]{0:T(1024)}, u32[]{:S(2)}) copy-start(f32[1024]{0:T(1024)} %param.4) | copy-start | bytes 12292
where the time goes:
time: 34.4 us; the launch traced here: 34.2 us
  Pallas kernels  29.7 us (86%)
  local copies, waits for them, and re-layouts  3.89 us (11%)
  between operations  0.65 us (2%)
    pallas_call x1, Pallas kernels, per_device(): pl.pallas_call(kernel, out_shape=(jax.ShapeDtypeStruct((2, 8, 8, 64), F32...  29.7 us
    unnamed x7, local copies, waits for them, and re-layouts  3.89 us

commit v1 on v0

v1 whole, which is shorter than its diff:
```python
import jax
import jax.numpy as jnp
from jax import lax
from jax.experimental import pallas as pl
from jax.experimental.pallas import tpu as pltpu
from jax.sharding import PartitionSpec as P

ITERS = 4
AHEAD = 8
FIRST = 2
HELLO = 3
F32 = jnp.float32
BF16 = jnp.bfloat16
MESH = pl.DeviceIdType.MESH


def split3(value):
    first = value.astype(BF16).astype(F32)
    rest = value - first
    second = rest.astype(BF16).astype(F32)
    return first, second, rest - second


def iota(shape, dim):
    return lax.broadcasted_iota(jnp.int32, shape, dim)


def order(own):
    x = own // 2
    core = own % 2
    sign = 1 - 2 * ((3 - x) // 3)
    near = [(2, 0), (2, 1), (sign, 0), (sign, 1), (-sign, 0), (-sign, 1), (0, 1), (0, 0)]
    return [((x + dx + 4) % 4) * 2 + (core + dc) % 2 for dx, dc in near]


def opening(data, out, sem):
    freq = order(lax.axis_index("pts") % 8)
    copies = [
        pltpu.make_async_copy(data.at[:, freq[s]], out.at[s], sem.at[s]) for s in range(FIRST)
    ]
    for copy in copies:
        copy.start()
    for copy in copies:
        copy.wait()


def kernel(
    data, weight, start, first, basis_out, spec_out, modes_out,
    wbuf, sbuf, xbuf, pbuf, rbuf, gbuf, tbuf, vbuf, abuf, rmat,
    in_sem, load_sem, ps_sem, pr_sem, gs_sem, ts_sem, tr_sem, vs_sem, vr_sem, as_sem, ar_sem, ready,
    *ybuf,
):
    me = lax.axis_index("pts")
    line = lax.axis_index("freq")
    z = me // 8
    own = me % 8
    x = own // 2
    core = own % 2
    freq = order(own)
    goal = z * 8
    top = z // 3
    everyone = [
        zt * 8 + ((x + dx) % 4) * 2 + (core + dc) % 2
        for zt in (0, 1, 2, 3) for dx in (2, 1, 3, 0) for dc in (1, 0)
    ][:31]
    lines = [(line + d) % 4 for d in (2, 1, 3)]

    def load(s):
        return pltpu.make_async_copy(data.at[:, freq[s]], xbuf.at[s - FIRST], load_sem.at[s])

    get_weight = pltpu.make_async_copy(weight, wbuf, in_sem.at[0])
    get_start = pltpu.make_async_copy(start.at[:, own], sbuf, in_sem.at[1])
    get_weight.start()
    for s in range(FIRST, 8):
        load(s).start()
    get_start.start()

    barrier = pltpu.get_barrier_semaphore()

    def greet(peer):
        pl.semaphore_signal(barrier, inc=1, device_id={"pts": peer}, device_id_type=MESH)

    for s in range(7):
        greet(z * 8 + freq[s])

    @pl.when(z < 3)
    def _():
        for f in range(8):
            greet(24 + f)

    @pl.when(z == 3)
    def _():
        for peer in lines:
            pl.semaphore_signal(barrier, inc=1, device_id={"freq": peer}, device_id_type=MESH)

    get_weight.wait()
    w = wbuf[...]
    root = jnp.sqrt(w)
    low = iota((1, 128), 1) < 64
    half = jnp.where(low, 1.0, -1.0).astype(F32)

    def split(s, hook):
        if s >= FIRST:
            load(s).wait()
        for c in range(3):
            if c == 1:
                hook()
            span = pl.ds(c * 1024, 1024)
            for part in range(2):
                for r in range(0, 64, 16):
                    y = (first[s, part, c, pl.ds(r, 16)] if s < FIRST else xbuf[s - FIRST, part, c, pl.ds(r, 16)]) * root
                    hi = y.astype(BF16)
                    lo = (y - hi.astype(F32)).astype(BF16)
                    ybuf[s][pl.ds(part * 64 + r, 16), span] = hi
                    ybuf[s][pl.ds(128 + part * 64 + r, 16), span] = lo

    def product(s):
        total = None
        for k in range(2):
            both = ybuf[s][:, pl.ds(k * 1536, 1536)]
            m = lax.dot_general(both, both, (((1,), (1,)), ((), ())), preferred_element_type=F32)
            m = (m[:128, :128] + m[128:, 128:]) + (m[:128, 128:] + m[128:, :128])
            total = m if total is None else total + m
        return total

    def packed(m):
        top, bottom = m[:64], m[64:]
        straight = top + half * pltpu.roll(bottom, 64, 1)
        swapped = pltpu.roll(top, 64, 1) - half * bottom
        row = iota((64, 128), 0)
        col = iota((64, 128), 1) % 64
        upper = jnp.where(low == (col >= row), straight, swapped)
        return jnp.where(low, upper[:32], upper[32:])

    def send_product(s):
        return pltpu.make_async_remote_copy(
            src_ref=pbuf.at[s], dst_ref=rbuf.at[own], send_sem=ps_sem.at[s], recv_sem=pr_sem.at[own],
            device_id={"pts": goal + freq[s]}, device_id_type=MESH)

    def take_product(at):
        return pltpu.make_async_remote_copy(
            src_ref=pbuf.at[0], dst_ref=rbuf.at[at], send_sem=ps_sem.at[0], recv_sem=pr_sem.at[at],
            device_id={"pts": goal + freq[0]}, device_id_type=MESH)

    def send_row():
        return pltpu.make_async_remote_copy(
            src_ref=gbuf, dst_ref=rbuf.at[8 + z], send_sem=gs_sem.at[0], recv_sem=pr_sem.at[8 + z],
            device_id={"pts": 24 + own}, device_id_type=MESH)

    before = None

    def passed(s):
        if not s:
            return
        pbuf[s - 1] = packed(before)
        if s == HELLO:
            pl.semaphore_wait(barrier, 7 + 27 * top)

            @pl.when(z == 3)
            def _():
                for peer in (0, 8, 16):
                    pl.semaphore_signal(
                        ready, inc=1, device_id={"pts": peer + own}, device_id_type=MESH)
        for k in range(s) if s == HELLO else [s - 1] if s > HELLO else []:
            send_product(k).start()

    for s in range(8):
        split(s, lambda: passed(s))
        before = product(s)
    pbuf[7] = packed(before)

    def send_trace(i):
        return pltpu.make_async_remote_copy(
            src_ref=tbuf.at[line], dst_ref=tbuf.at[line], send_sem=ts_sem.at[i], recv_sem=tr_sem.at[line],
            device_id={"freq": lines[i]}, device_id_type=MESH)

    def take_trace(i):
        return pltpu.make_async_remote_copy(
            src_ref=tbuf.at[line], dst_ref=tbuf.at[lines[i]], send_sem=ts_sem.at[i], recv_sem=tr_sem.at[lines[i]],
            device_id={"freq": lines[i]}, device_id_type=MESH)

    def send_basis(i):
        return pltpu.make_async_remote_copy(
            src_ref=vbuf.at[own], dst_ref=vbuf.at[own], send_sem=vs_sem.at[i], recv_sem=vr_sem.at[own],
            device_id={"pts": everyone[i]}, device_id_type=MESH)

    def take_basis(s):
        return pltpu.make_async_remote_copy(
            src_ref=vbuf.at[own], dst_ref=vbuf.at[freq[s]], send_sem=vs_sem.at[0], recv_sem=vr_sem.at[freq[s]],
            device_id={"pts": 24 + freq[s]}, device_id_type=MESH)

    def send_aux(i):
        return pltpu.make_async_remote_copy(
            src_ref=abuf.at[own], dst_ref=abuf.at[own], send_sem=as_sem.at[i], recv_sem=ar_sem.at[own],
            device_id={"pts": everyone[i]}, device_id_type=MESH)

    def take_aux(s):
        return pltpu.make_async_remote_copy(
            src_ref=abuf.at[own], dst_ref=abuf.at[freq[s]], send_sem=as_sem.at[0], recv_sem=ar_sem.at[freq[s]],
            device_id={"pts": 24 + freq[s]}, device_id_type=MESH)

    def applied(vectors):
        pieces = []
        for v in vectors:
            pieces.extend(split3(v))
        while len(pieces) % 2:
            pieces.append(jnp.zeros((8, 128), F32))
        left = jnp.concatenate(pieces, axis=0).astype(BF16)
        out = jnp.dot(jnp.concatenate([left, left], axis=1), rmat[...], preferred_element_type=F32)
        results = []
        for i in range(len(vectors)):
            parts = [out[24 * i + 8 * k : 24 * i + 8 * k + 8] for k in range(3)]
            small = (parts[2][:, :128] + parts[0][:, 128:]) + (parts[1][:, 128:] + parts[2][:, 128:])
            results.append(parts[0][:, :128] + (parts[1][:, :128] + small))
        return results

    get_start.wait()

    @pl.when(z < 3)
    def _():
        total = pbuf[7]
        for s in range(7):
            take_product(freq[s]).wait_recv()
            total = total + rbuf[freq[s]]
        gbuf[...] = total
        pl.semaphore_wait(ready, 1)
        send_row().start()
        send_row().wait_send()

    @pl.when(z == 3)
    def _():
        total = pbuf[7]
        for s in range(7):
            take_product(freq[s]).wait_recv()
            total = total + rbuf[freq[s]]
        for at in (8, 9, 10):
            take_product(at).wait_recv()
            total = total + rbuf[at]
        gram = total * (1.0 / 98304.0)
        turned = pltpu.roll(gram, 64, 1)
        upper = jnp.concatenate([jnp.where(low, gram, turned), jnp.where(low, turned, gram)], axis=0)
        flipped = jnp.concatenate([upper, upper], axis=0).T[:64]
        row = iota((64, 128), 0)
        col = iota((64, 128), 1) % 64
        real = jnp.where(col >= row, upper, flipped)
        imag = jnp.where(col < row, upper, jnp.where(col > row, -flipped, 0.0))
        full = jnp.concatenate([jnp.where(low, real, -imag), jnp.where(low, imag, real)], axis=0)
        r0, r1, r2 = split3(full)
        rmat[pl.ds(0, 128), pl.ds(0, 128)] = r0.astype(BF16)
        rmat[pl.ds(128, 128), pl.ds(0, 128)] = r1.astype(BF16)
        rmat[pl.ds(0, 128), pl.ds(128, 128)] = r2.astype(BF16)
        rmat[pl.ds(128, 128), pl.ds(128, 128)] = jnp.zeros((128, 128), BF16)

        diag = jnp.where((col == row) & low, upper, 0.0)
        trace = jnp.sum(jnp.sum(diag, axis=1, keepdims=True), axis=0, keepdims=True)
        tbuf[line] = jnp.broadcast_to(trace, (8, 128))
        for i in range(3):
            send_trace(i).start()

        rank = iota((8, 128), 0)
        v = jnp.concatenate([sbuf[0], sbuf[1]], axis=1)
        iv = pltpu.roll(v, 64, 1) * -half
        for step in range(ITERS):
            zv, wv = applied([v, iv])
            scale = jnp.zeros((8, 128), F32)
            for j in range(8):
                zj = jnp.broadcast_to(zv[j : j + 1], (8, 128))
                wj = jnp.broadcast_to(wv[j : j + 1], (8, 128))
                dot_real = jnp.broadcast_to(jnp.sum(zj * zv, axis=1, keepdims=True), (8, 128))
                norm = jnp.broadcast_to(dot_real[j : j + 1], (8, 128))
                factor = lax.rsqrt(norm * (1.0 / 64) + 1e-06)
                scale = jnp.where(rank == j, factor, scale)
                if j < 7:
                    dot_imag = jnp.broadcast_to(jnp.sum(wj * zv, axis=1, keepdims=True), (8, 128))
                    inverse = jnp.where(rank > j, factor * factor * (1.0 / 64), 0.0)
                    coef_real = dot_real * inverse
                    coef_imag = dot_imag * inverse
                    zv, wv = (
                        zv - (coef_real * zj + coef_imag * wj),
                        wv - (coef_real * wj - coef_imag * zj),
                    )
            v = zv * scale
            iv = wv * scale
        vbuf[own] = v
        for i in range(31):
            send_basis(i).start()

        (zv,) = applied([v])
        rayleigh = jnp.sum(v * zv, axis=1, keepdims=True) * (1.0 / 64)
        spread = jnp.sum(jnp.where(rank == iota((8, 128), 1), rayleigh, 0.0), axis=0, keepdims=True)
        for i in (1, 2, 0):
            take_trace(i).wait_recv()
        group = (tbuf[0] + tbuf[1]) + (tbuf[2] + tbuf[3])
        abuf[own] = jnp.where(rank == 0, spread, group)
        for i in range(31):
            send_aux(i).start()
        for i in range(3):
            send_trace(i).wait_send()

    undo = lax.rsqrt(w) * (1.0 / 64)

    for s in reversed(range(8)):
        if s < 7:
            take_basis(s).wait_recv()
        else:
            @pl.when(z < 3)
            def _():
                take_basis(7).wait_recv()
        vec = vbuf[freq[s]]
        other = pltpu.roll(vec, 64, 1)
        basis_out[0, freq[s]] = vec[:, :64]
        basis_out[1, freq[s]] = other[:, :64]
        left = jnp.concatenate([vec * half, other], axis=0)
        left_hi = left.astype(BF16)
        left_lo = (left - left_hi.astype(F32)).astype(BF16)
        left = jnp.concatenate([left_hi, left_lo], axis=0)
        left = jnp.concatenate([left, left], axis=1)
        for k in range(6):
            c, at = k // 2, k % 2 * 512
            out = jnp.dot(left, ybuf[s][:, pl.ds(k * 512, 512)], preferred_element_type=F32)
            out = (out[:16] + out[16:]) * undo[:, at : at + 512]
            modes_out[0, freq[s], c, :, pl.ds(at, 512)] = out[:8]
            modes_out[1, freq[s], c, :, pl.ds(at, 512)] = out[8:]

    for s in range(7):
        take_aux(s).wait_recv()

    @pl.when(z < 3)
    def _():
        take_aux(7).wait_recv()

    total = jnp.zeros((1, 128), F32)
    for f in range(8):
        total = total + abuf[f, 1:2]
    for f in range(8):
        spec_out[pl.ds(f, 1), :] = (abuf[f, 0:1] * 2048.0 / total)[:, :8]

    for s in range(7):
        send_product(s).wait_send()

    @pl.when(z == 3)
    def _():
        for i in range(31):
            send_basis(i).wait_send()
            send_aux(i).wait_send()


def writer(basis_in, spec_in, modes_in, basis_out, spec_out, modes_out, sem):
    copies = [
        pltpu.make_async_copy(modes_in, modes_out, sem.at[0]),
        pltpu.make_async_copy(basis_in, basis_out, sem.at[1]),
        pltpu.make_async_copy(spec_in, spec_out, sem.at[2]),
    ]
    for copy in copies:
        copy.start()
    for copy in copies:
        copy.wait()


def per_device(data, quad_weight, basis):
    data = jnp.transpose(data, (0, 1, 3, 2, 4))
    basis = jnp.transpose(basis, (0, 1, 3, 2))
    vmem = pl.BlockSpec(memory_space=pltpu.VMEM)
    hbm = pl.BlockSpec(memory_space=pltpu.HBM)
    dma = pltpu.SemaphoreType.DMA
    shapes = (
        jax.ShapeDtypeStruct((2, 8, 8, 64), F32),
        jax.ShapeDtypeStruct((8, 8), F32),
        jax.ShapeDtypeStruct((2, 8, 3, 8, 1024), F32),
    )
    first = pl.pallas_call(
        opening,
        out_shape=jax.ShapeDtypeStruct((FIRST, 2, 3, 64, 1024), F32),
        in_specs=[hbm],
        out_specs=vmem,
        scratch_shapes=[dma((FIRST,))],
        compiler_params=pltpu.CompilerParams(vmem_limit_bytes=48 * 1024 * 1024),
        cost_estimate=pl.CostEstimate(flops=10**9, bytes_accessed=6 * 10**6, transcendentals=0),
        name="opening",
    )(data)
    results = pl.pallas_call(
        kernel,
        out_shape=shapes,
        in_specs=[hbm, hbm, hbm, vmem],
        out_specs=(vmem, vmem, vmem),
        scratch_shapes=[
            pltpu.VMEM((1, 1024), F32),
            pltpu.VMEM((2, 8, 64), F32),
            pltpu.VMEM((8 - FIRST, 2, 3, 64, 1024), F32),
            pltpu.VMEM((8, 32, 128), F32),
            pltpu.VMEM((11, 32, 128), F32),
            pltpu.VMEM((32, 128), F32),
            pltpu.VMEM((4, 8, 128), F32),
            pltpu.VMEM((8, 8, 128), F32),
            pltpu.VMEM((8, 8, 128), F32),
            pltpu.VMEM((256, 256), BF16),
            dma((2,)), dma((8,)), dma((8,)), dma((11,)), dma((1,)),
            dma((3,)), dma((4,)), dma((31,)), dma((8,)), dma((31,)), dma((8,)),
            pltpu.SemaphoreType.REGULAR,
            *[pltpu.VMEM((256, 3072), BF16) for _ in range(8)],
        ],
        compiler_params=pltpu.CompilerParams(
            collective_id=0, has_side_effects=True, vmem_limit_bytes=48 * 1024 * 1024
        ),
        name="spod",
    )(data, quad_weight.reshape(1, -1), basis, first)
    basis_out, spectrum, modes = pl.pallas_call(
        writer,
        out_shape=shapes,
        in_specs=[vmem, vmem, vmem],
        out_specs=(hbm, hbm, hbm),
        scratch_shapes=[dma((3,))],
        compiler_params=pltpu.CompilerParams(vmem_limit_bytes=4 * 1024 * 1024),
        name="writer",
    )(*results)
    return (
        jnp.transpose(basis_out, (0, 1, 3, 2)),
        spectrum,
        jnp.transpose(modes, (0, 1, 3, 2, 4)),
    )


def solution(mesh):
    in_specs = (P(None, "freq", None, None, "pts"), P("pts"), P(None, "freq", None, None))
    out_specs = (P(None, "freq", None, None), P("freq", None), P(None, "freq", None, None, "pts"))
    return jax.shard_map(
        per_device, mesh=mesh, in_specs=in_specs, out_specs=out_specs, check_vma=False
    )
```

time: 34.4 us -> 28.5 us (0.83)
  local copies, waits for them, and re-layouts: 3.89 us -> 0.01 us
  Pallas kernels: 29.7 us -> 27.7 us
    unnamed x7 -> x4, local copies, waits for them, and re-layouts: 3.89 us -> 0.01 us
    pallas_call x1 -> x3, Pallas kernels: 29.7 us -> 27.7 us  [the longest x1 24.6 us: per_device(): pl.pallas_call(kernel, out_shape=shapes, in_specs=[hbm, hbm, hbm, vmem],...]
where the time goes in v1:
time: 28.5 us; the launch traced here: 28.4 us
  Pallas kernels  27.7 us (97%)
  between operations  0.68 us (2%)
    pallas_call x1, Pallas kernels, per_device(): pl.pallas_call(kernel, out_shape=shapes, in_specs=[hbm, hbm, hbm, vmem],...  24.6 us
    pallas_call x1, Pallas kernels, per_device(): pl.pallas_call(opening, out_shape=jax.ShapeDtypeStruct((FIRST, 2, 3, 64,...  1.93 us
    pallas_call x1, Pallas kernels, per_device(): pl.pallas_call(writer, out_shape=shapes, in_specs=[vmem, vmem, vmem], out...  1.18 us

profile of v1, /device:TPU:1, one launch (start us, length us, event | category | flops | bytes accessed | tf_op | source)
XLA Modules:
  0.0 28.4 jit_solution(16690471230806577487)
XLA Ops:
  0.6 0.0 copy-start
  0.6 0.0 copy-start.1
  0.7 1.9 %opening.1.first = f32[2,2,3,64,1024]{4,3,2,1,0:T(8,128)S(1)} custom-call(f32[2,8,3,64,1024]{4,3,2,1,0:T(8,128)} %bitcast.7), custom_call_target="tpu_custom_call" | custom-call | flops 1000000000 | bytes 6000000 | tf_op jit(solution)/shard_map/opening/pallas_call | solution.py:371
  2.6 0.0 copy-done
  2.6 0.0 copy-done.1
  2.6 24.6 %spod.1 = (f32[2,8,8,64]{3,2,1,0:T(8,128)S(1)}, f32[8,8]{1,0:T(8,128)S(1)}, f32[2,8,3,8,1024]{4,3,2,1,0:T(8,128)S(1)}) custom-call(f32[2,8,3,64,1024]{4,3,2,1,0:T(8,128)} %bitcast.8, f32[1,1024]{1,0:T(1,128)S(1)} %bitcast.6, f32[2,8,8,64]{3,2,1,0:T(8,128)S(1)} %bitcast.5, f32[2,2,3,64,1024]{4,3,2,1,0:T(8,128)S(1)} %opening.1.first), custom_call_target="tpu_custom_call" | custom-call | tf_op jit(solution)/shard_map/spod/pallas_call | solution.py:381
  27.2 1.2 %writer.1 = (f32[2,8,8,64]{3,2,1,0:T(8,128)}, f32[8,8]{1,0:T(8,128)}, f32[2,8,3,8,1024]{4,3,2,1,0:T(8,128)}) custom-call(f32[2,8,8,64]{3,2,1,0:T(8,128)S(1)} %get-tuple-element.9.basis_in, f32[8,8]{1,0:T(8,128)S(1)} %get-tuple-element.10.spec_in, f32[2,8,3,8,1024]{4,3,2,1,0:T(8,128)S(1)} %get-tuple-element.11.modes_in), custom_call_target="tpu_custom_call" | custom-call | tf_op jit(solution)/shard_map/writer/pallas_call | solution.py:407
Async XLA Ops:
  0.6 2.0 %copy-start = (f32[2,8,64,8]{2,3,1,0:T(8,128)S(1)}, f32[2,8,64,8]{2,3,1,0:T(8,128)}, u32[]{:S(2)}) copy-start(f32[2,8,64,8]{2,3,1,0:T(8,128)} %param.5) | copy-start | bytes 98308
  0.6 2.0 %copy-start.1 = (f32[1024]{0:T(1024)S(1)}, f32[1024]{0:T(1024)}, u32[]{:S(2)}) copy-start(f32[1024]{0:T(1024)} %param.4) | copy-start | bytes 12292

commit v2 on v1

--- a/solution.py
+++ b/solution.py
@@ -46,8 +46,8 @@
 
 def kernel(
     data, weight, start, first, basis_out, spec_out, modes_out,
-    wbuf, sbuf, xbuf, pbuf, rbuf, gbuf, tbuf, vbuf, abuf, rmat,
-    in_sem, load_sem, ps_sem, pr_sem, gs_sem, ts_sem, tr_sem, vs_sem, vr_sem, as_sem, ar_sem, ready,
+    xbuf, pbuf, rbuf, gbuf, tbuf, vbuf, abuf, rmat,
+    load_sem, ps_sem, pr_sem, gs_sem, ts_sem, tr_sem, vs_sem, vr_sem, as_sem, ar_sem, ready,
     *ybuf,
 ):
     me = lax.axis_index("pts")
@@ -59,21 +59,16 @@
     freq = order(own)
     goal = z * 8
     top = z // 3
-    everyone = [
-        zt * 8 + ((x + dx) % 4) * 2 + (core + dc) % 2
-        for zt in (0, 1, 2, 3) for dx in (2, 1, 3, 0) for dc in (1, 0)
-    ][:31]
+    everyone = list(range(24)) + [
+        24 + ((x + dx) % 4) * 2 + (core + dc) % 2 for dx in (2, 1, 3, 0) for dc in (1, 0)
+    ][:7]
     lines = [(line + d) % 4 for d in (2, 1, 3)]
 
     def load(s):
         return pltpu.make_async_copy(data.at[:, freq[s]], xbuf.at[s - FIRST], load_sem.at[s])
 
-    get_weight = pltpu.make_async_copy(weight, wbuf, in_sem.at[0])
-    get_start = pltpu.make_async_copy(start.at[:, own], sbuf, in_sem.at[1])
-    get_weight.start()
     for s in range(FIRST, 8):
         load(s).start()
-    get_start.start()
 
     barrier = pltpu.get_barrier_semaphore()
 
@@ -93,8 +88,7 @@
         for peer in lines:
             pl.semaphore_signal(barrier, inc=1, device_id={"freq": peer}, device_id_type=MESH)
 
-    get_weight.wait()
-    w = wbuf[...]
+    w = weight[...]
     root = jnp.sqrt(w)
     low = iota((1, 128), 1) < 64
     half = jnp.where(low, 1.0, -1.0).astype(F32)
@@ -214,7 +208,6 @@
             results.append(parts[0][:, :128] + (parts[1][:, :128] + small))
         return results
 
-    get_start.wait()
 
     @pl.when(z < 3)
     def _():
@@ -258,10 +251,14 @@
             send_trace(i).start()
 
         rank = iota((8, 128), 0)
-        v = jnp.concatenate([sbuf[0], sbuf[1]], axis=1)
+        v = jnp.concatenate([start[0, own], start[1, own]], axis=1)
         iv = pltpu.roll(v, 64, 1) * -half
+        scale = None
+        zv, wv = v, iv
         for step in range(ITERS):
-            zv, wv = applied([v, iv])
+            zv, wv = applied([zv, wv])
+            if scale is not None:
+                zv, wv = zv * scale, wv * scale
             scale = jnp.zeros((8, 128), F32)
             for j in range(8):
                 zj = jnp.broadcast_to(zv[j : j + 1], (8, 128))
@@ -279,8 +276,7 @@
                         zv - (coef_real * zj + coef_imag * wj),
                         wv - (coef_real * wj - coef_imag * zj),
                     )
-            v = zv * scale
-            iv = wv * scale
+        v = zv * scale
         vbuf[own] = v
         for i in range(31):
             send_basis(i).start()
@@ -291,7 +287,7 @@
         for i in (1, 2, 0):
             take_trace(i).wait_recv()
         group = (tbuf[0] + tbuf[1]) + (tbuf[2] + tbuf[3])
-        abuf[own] = jnp.where(rank == 0, spread, group)
+        abuf[own] = jnp.where(low, spread, group[:1])
         for i in range(31):
             send_aux(i).start()
         for i in range(3):
@@ -329,11 +325,11 @@
     def _():
         take_aux(7).wait_recv()
 
-    total = jnp.zeros((1, 128), F32)
+    total = jnp.zeros((1, 8), F32)
     for f in range(8):
-        total = total + abuf[f, 1:2]
+        total = total + abuf[f, :, 64:72]
     for f in range(8):
-        spec_out[pl.ds(f, 1), :] = (abuf[f, 0:1] * 2048.0 / total)[:, :8]
+        spec_out[pl.ds(f, 1), :] = abuf[f, :, :8] * 2048.0 / total
 
     for s in range(7):
         send_product(s).wait_send()
@@ -381,20 +377,18 @@
     results = pl.pallas_call(
         kernel,
         out_shape=shapes,
-        in_specs=[hbm, hbm, hbm, vmem],
+        in_specs=[hbm, vmem, vmem, vmem],
         out_specs=(vmem, vmem, vmem),
         scratch_shapes=[
-            pltpu.VMEM((1, 1024), F32),
-            pltpu.VMEM((2, 8, 64), F32),
             pltpu.VMEM((8 - FIRST, 2, 3, 64, 1024), F32),
             pltpu.VMEM((8, 32, 128), F32),
             pltpu.VMEM((11, 32, 128), F32),
             pltpu.VMEM((32, 128), F32),
             pltpu.VMEM((4, 8, 128), F32),
             pltpu.VMEM((8, 8, 128), F32),
-            pltpu.VMEM((8, 8, 128), F32),
+            pltpu.VMEM((8, 1, 128), F32),
             pltpu.VMEM((256, 256), BF16),
-            dma((2,)), dma((8,)), dma((8,)), dma((11,)), dma((1,)),
+            dma((8,)), dma((8,)), dma((11,)), dma((1,)),
             dma((3,)), dma((4,)), dma((31,)), dma((8,)), dma((31,)), dma((8,)),
             pltpu.SemaphoreType.REGULAR,
             *[pltpu.VMEM((256, 3072), BF16) for _ in range(8)],

time: 28.5 us -> 28.1 us (0.986)
  Pallas kernels: 27.7 us -> 27.3 us
    pallas_call x1, Pallas kernels: 24.6 us -> 24.2 us  [per_device(): pl.pallas_call(kernel, out_shape=shapes, in_specs=[hbm, vmem, vmem, vmem]...]
where the time goes in v2:
time: 28.1 us; the launch traced here: 28 us
  Pallas kernels  27.3 us (97%)
  between operations  0.68 us (2%)
    pallas_call x1, Pallas kernels, per_device(): pl.pallas_call(kernel, out_shape=shapes, in_specs=[hbm, vmem, vmem, vmem]...  24.2 us
    pallas_call x1, Pallas kernels, per_device(): pl.pallas_call(opening, out_shape=jax.ShapeDtypeStruct((FIRST, 2, 3, 64,...  1.93 us
    pallas_call x1, Pallas kernels, per_device(): pl.pallas_call(writer, out_shape=shapes, in_specs=[vmem, vmem, vmem], out...  1.18 us

profile of v2, /device:TPU:1, one launch (start us, length us, event | category | flops | bytes accessed | tf_op | source)
XLA Modules:
  0.0 28.0 jit_solution(18338992250879680054)
XLA Ops:
  0.6 0.0 copy-start
  0.6 0.0 copy-start.1
  0.7 1.9 %opening.1.first = f32[2,2,3,64,1024]{4,3,2,1,0:T(8,128)S(1)} custom-call(f32[2,8,3,64,1024]{4,3,2,1,0:T(8,128)} %bitcast.7), custom_call_target="tpu_custom_call" | custom-call | flops 1000000000 | bytes 6000000 | tf_op jit(solution)/shard_map/opening/pallas_call | solution.py:367
  2.6 0.0 copy-done
  2.6 0.0 copy-done.1
  2.6 24.2 %spod.1 = (f32[2,8,8,64]{3,2,1,0:T(8,128)S(1)}, f32[8,8]{1,0:T(8,128)S(1)}, f32[2,8,3,8,1024]{4,3,2,1,0:T(8,128)S(1)}) custom-call(f32[2,8,3,64,1024]{4,3,2,1,0:T(8,128)} %bitcast.8, f32[1,1024]{1,0:T(1,128)S(1)} %bitcast.6, f32[2,8,8,64]{3,2,1,0:T(8,128)S(1)} %bitcast.5, f32[2,2,3,64,1024]{4,3,2,1,0:T(8,128)S(1)} %opening.1.first), custom_call_target="tpu_custom_call" | custom-call | tf_op jit(solution)/shard_map/spod/pallas_call | solution.py:377
  26.8 1.2 %writer.1 = (f32[2,8,8,64]{3,2,1,0:T(8,128)}, f32[8,8]{1,0:T(8,128)}, f32[2,8,3,8,1024]{4,3,2,1,0:T(8,128)}) custom-call(f32[2,8,8,64]{3,2,1,0:T(8,128)S(1)} %get-tuple-element.9.basis_in, f32[8,8]{1,0:T(8,128)S(1)} %get-tuple-element.10.spec_in, f32[2,8,3,8,1024]{4,3,2,1,0:T(8,128)S(1)} %get-tuple-element.11.modes_in), custom_call_target="tpu_custom_call" | custom-call | tf_op jit(solution)/shard_map/writer/pallas_call | solution.py:401
Async XLA Ops:
  0.6 2.0 %copy-start = (f32[2,8,64,8]{2,3,1,0:T(8,128)S(1)}, f32[2,8,64,8]{2,3,1,0:T(8,128)}, u32[]{:S(2)}) copy-start(f32[2,8,64,8]{2,3,1,0:T(8,128)} %param.5) | copy-start | bytes 98308
  0.6 2.0 %copy-start.1 = (f32[1024]{0:T(1024)S(1)}, f32[1024]{0:T(1024)}, u32[]{:S(2)}) copy-start(f32[1024]{0:T(1024)} %param.4) | copy-start | bytes 12292

commit v3 on v2

--- a/solution.py
+++ b/solution.py
@@ -276,13 +276,13 @@
                         zv - (coef_real * zj + coef_imag * wj),
                         wv - (coef_real * wj - coef_imag * zj),
                     )
+        (out,) = applied([zv])
         v = zv * scale
         vbuf[own] = v
         for i in range(31):
             send_basis(i).start()
 
-        (zv,) = applied([v])
-        rayleigh = jnp.sum(v * zv, axis=1, keepdims=True) * (1.0 / 64)
+        rayleigh = jnp.sum(v * (out * scale), axis=1, keepdims=True) * (1.0 / 64)
         spread = jnp.sum(jnp.where(rank == iota((8, 128), 1), rayleigh, 0.0), axis=0, keepdims=True)
         for i in (1, 2, 0):
             take_trace(i).wait_recv()
@@ -343,9 +343,11 @@
 
 def writer(basis_in, spec_in, modes_in, basis_out, spec_out, modes_out, sem):
     copies = [
-        pltpu.make_async_copy(modes_in, modes_out, sem.at[0]),
-        pltpu.make_async_copy(basis_in, basis_out, sem.at[1]),
-        pltpu.make_async_copy(spec_in, spec_out, sem.at[2]),
+        pltpu.make_async_copy(modes_in.at[part, pl.ds(4 * i, 4)], modes_out.at[part, pl.ds(4 * i, 4)], sem.at[2 * part + i])
+        for part in range(2) for i in range(2)
+    ] + [
+        pltpu.make_async_copy(basis_in, basis_out, sem.at[4]),
+        pltpu.make_async_copy(spec_in, spec_out, sem.at[5]),
     ]
     for copy in copies:
         copy.start()
@@ -403,7 +405,7 @@
         out_shape=shapes,
         in_specs=[vmem, vmem, vmem],
         out_specs=(hbm, hbm, hbm),
-        scratch_shapes=[dma((3,))],
+        scratch_shapes=[dma((6,))],
         compiler_params=pltpu.CompilerParams(vmem_limit_bytes=4 * 1024 * 1024),
         name="writer",
     )(*results)

time: 28.1 us -> 28.1 us (level)
  no operation moved by 1% of the time
where the time goes in v3:
time: 28.1 us; the launch traced here: 28 us
  Pallas kernels  27.3 us (97%)
  between operations  0.68 us (2%)
    pallas_call x1, Pallas kernels, per_device(): pl.pallas_call(kernel, out_shape=shapes, in_specs=[hbm, vmem, vmem, vmem]...  24.2 us
    pallas_call x1, Pallas kernels, per_device(): pl.pallas_call(opening, out_shape=jax.ShapeDtypeStruct((FIRST, 2, 3, 64,...  1.93 us
    pallas_call x1, Pallas kernels, per_device(): pl.pallas_call(writer, out_shape=shapes, in_specs=[vmem, vmem, vmem], out...  1.2 us

profile of v3, /device:TPU:1, one launch (start us, length us, event | category | flops | bytes accessed | tf_op | source)
XLA Modules:
  0.0 28.0 jit_solution(11979195301491429295)
XLA Ops:
  0.6 0.0 copy-start
  0.6 0.0 copy-start.1
  0.7 1.9 %opening.1.first = f32[2,2,3,64,1024]{4,3,2,1,0:T(8,128)S(1)} custom-call(f32[2,8,3,64,1024]{4,3,2,1,0:T(8,128)} %bitcast.7), custom_call_target="tpu_custom_call" | custom-call | flops 1000000000 | bytes 6000000 | tf_op jit(solution)/shard_map/opening/pallas_call | solution.py:369
  2.6 0.0 copy-done
  2.6 0.0 copy-done.1
  2.6 24.2 %spod.1 = (f32[2,8,8,64]{3,2,1,0:T(8,128)S(1)}, f32[8,8]{1,0:T(8,128)S(1)}, f32[2,8,3,8,1024]{4,3,2,1,0:T(8,128)S(1)}) custom-call(f32[2,8,3,64,1024]{4,3,2,1,0:T(8,128)} %bitcast.8, f32[1,1024]{1,0:T(1,128)S(1)} %bitcast.6, f32[2,8,8,64]{3,2,1,0:T(8,128)S(1)} %bitcast.5, f32[2,2,3,64,1024]{4,3,2,1,0:T(8,128)S(1)} %opening.1.first), custom_call_target="tpu_custom_call" | custom-call | tf_op jit(solution)/shard_map/spod/pallas_call | solution.py:379
  26.8 1.2 %writer.1 = (f32[2,8,8,64]{3,2,1,0:T(8,128)}, f32[8,8]{1,0:T(8,128)}, f32[2,8,3,8,1024]{4,3,2,1,0:T(8,128)}) custom-call(f32[2,8,8,64]{3,2,1,0:T(8,128)S(1)} %get-tuple-element.9.basis_in, f32[8,8]{1,0:T(8,128)S(1)} %get-tuple-element.10.spec_in, f32[2,8,3,8,1024]{4,3,2,1,0:T(8,128)S(1)} %get-tuple-element.11.modes_in), custom_call_target="tpu_custom_call" | custom-call | tf_op jit(solution)/shard_map/writer/pallas_call | solution.py:403
Async XLA Ops:
  0.6 2.0 %copy-start = (f32[2,8,64,8]{2,3,1,0:T(8,128)S(1)}, f32[2,8,64,8]{2,3,1,0:T(8,128)}, u32[]{:S(2)}) copy-start(f32[2,8,64,8]{2,3,1,0:T(8,128)} %param.5) | copy-start | bytes 98308
  0.6 2.0 %copy-start.1 = (f32[1024]{0:T(1024)S(1)}, f32[1024]{0:T(1024)}, u32[]{:S(2)}) copy-start(f32[1024]{0:T(1024)} %param.4) | copy-start | bytes 12292
